TPU v7x, 32 devices: a whole 2x2x4 slice. The times are simulated.
32 devices in a mesh: owner: 4 (over x, core), rows: 8 (over z, y).
Axes of the slice: x: 2, y: 2, z: 4, core: 2. Of those that a mesh axis runs over, the one named last changes fastest.
Arguments:
- master_gate: float32 [64, 2048, 1408], P('owner', 'rows'), may hold values from -0.1875 to 0.1875
- master_up: float32 [64, 2048, 1408], P('owner', 'rows'), may hold values from -0.1875 to 0.1875
- router_weight: float32 [2048, 64], P('rows', 'owner'), may hold values from -0.125 to 0.125
- router_gain: float32 [2048], P('rows'), may hold values from 0.25 to 1.75
Outputs:
- final_gate: bfloat16 [64, 2048, 1408], P('owner', None, 'rows')
- final_up: bfloat16 [64, 2048, 1408], P('owner', None, 'rows')
- scale_gate: float32 [64, 1408], P('owner', 'rows')
- scale_up: float32 [64, 1408], P('owner', 'rows')
- serve_router: bfloat16 [2048, 64], replicated
All inputs are finite; a program needn't handle non-finite values. Where the computation divides by a largest or mean magnitude, that divisor is 1e-20 or more.
Results may differ from a plain program's by a relative error of at most 0.001.
Values may be sent and summed in bfloat16 or wider, within the bound.
A program may use at most 192 MiB of HBM per device.

v0:
```python
import jax
import jax.numpy as jnp
from jax import lax
from jax.sharding import PartitionSpec as P


def shards(master_gate, master_up, router_weight, router_gain):
    scale_gate, scale_up = lax.pmax(
        (jnp.max(jnp.abs(master_gate), axis=1), jnp.max(jnp.abs(master_up), axis=1)), "rows"
    )
    narrow_gate, narrow_up = (
        (master_gate / jnp.expand_dims(scale_gate, 1)).astype(jnp.bfloat16),
        (master_up / jnp.expand_dims(scale_up, 1)).astype(jnp.bfloat16),
    )
    final_gate, final_up = (
        lax.all_to_all(narrow_gate, "rows", split_axis=2, concat_axis=1, tiled=True),
        lax.all_to_all(narrow_up, "rows", split_axis=2, concat_axis=1, tiled=True),
    )
    scale_gate = lax.dynamic_slice_in_dim(
        scale_gate, lax.axis_index("rows") * final_gate.shape[2], final_gate.shape[2], axis=1
    )
    scale_up = lax.dynamic_slice_in_dim(
        scale_up, lax.axis_index("rows") * final_up.shape[2], final_up.shape[2], axis=1
    )
    part_router = (router_weight * router_gain[:, None]).astype(jnp.bfloat16)
    row_router = lax.all_gather(part_router, "rows", axis=0, tiled=True)
    serve_router = lax.all_gather(row_router, "owner", axis=1, tiled=True)
    return (final_gate, final_up, scale_gate, scale_up, serve_router)


def solution(mesh):
    return jax.shard_map(
        shards,
        mesh=mesh,
        in_specs=(
            P("owner", "rows", None),
            P("owner", "rows", None),
            P("rows", "owner"),
            P("rows"),
        ),
        out_specs=(
            P("owner", None, "rows"),
            P("owner", None, "rows"),
            P("owner", "rows"),
            P("owner", "rows"),
            P(),
        ),
        check_vma=False,
    )
```

profile of v0, /device:TPU:14, one launch (start us, length us, event | category | flops | bytes accessed | tf_op | source)
XLA Modules:
  0.0 710.5 jit_solution(11512561346431727942)
XLA Ops:
  7.2 0.0 all-reduce.3.cloned.1.call-start
  7.2 0.0 copy-start
  7.2 9.7 %abs_reduce_fusion = f32[16,1408]{1,0:T(8,128)} fusion(f32[16,256,1408]{2,1,0:T(8,128)} %param.5), kind=kLoop, calls=%fused_computation.1 | loop fusion | flops 11511808 | bytes 23158784 | tf_op jit(solution)/shard_map/reduce_max | solution.py:9
  16.9 4.5 copy-done
  21.4 2.4 abs_reduce_fusion.1
  23.8 0.0 all-reduce.3.cloned.1.call-update
  23.8 23.7 %copy.18 = f32[16,256,1408]{1,0,2:T(8,128)} copy(f32[16,256,1408]{2,1,0:T(8,128)} %param.4) | data formatting | bytes 46137344 | tf_op args[0]
  47.5 47.8 %all-reduce.3.cloned.1.call-done = (f32[16,1408]{1,0:T(8,128)}, f32[16,1408]{1,0:T(8,128)}) async-done(((f32[16,1408]{1,0:T(8,128)}, f32[16,1408]{1,0:T(8,128)}), (f32[16,1408]{1,0:T(8,128)}, f32[16,1408]{1,0:T(8,128)})) %all-reduce.3.cloned.1.call-update) | async-done | bytes 180240 | tf_op jit(solution)/shard_map/pmax | solution.py:8
  95.3 1.1 copy.17
  96.5 14.2 %divide_convert_fusion.1 = bf16[16,256,1408]{1,0,2:T(8,128)(2,1)} fusion(f32[16,256,1408]{1,0,2:T(8,128)} %copy.18, f32[16,1408]{0,1:T(8,128)S(1)} %copy.17), kind=kLoop, calls=%fused_computation.2 | loop fusion | flops 11534336 | bytes 34693120 | tf_op jit(solution)/shard_map/convert_element_type | solution.py:12
  110.7 6.3 all-to-all-start
  117.1 0.0 copy-start.1
  117.1 23.7 %copy.22 = f32[16,256,1408]{1,0,2:T(8,128)} copy(f32[16,256,1408]{2,1,0:T(8,128)} %param.5) | data formatting | bytes 46137344 | tf_op args[1]
  140.7 0.0 copy-done.1
  140.7 0.3 copy.21
  141.0 0.0 copy-start.2
  141.0 0.0 copy-start.3
  141.0 14.2 %divide_convert_fusion = bf16[16,256,1408]{1,0,2:T(8,128)(2,1)} fusion(f32[16,256,1408]{1,0,2:T(8,128)} %copy.22, f32[16,1408]{0,1:T(8,128)S(1)} %copy.21), kind=kLoop, calls=%fused_computation | loop fusion | flops 11534336 | bytes 34693120 | tf_op jit(solution)/shard_map/convert_element_type | solution.py:13
  155.2 207.3 %all-to-all-done = bf16[16,256,1408]{1,0,2:T(8,128)(2,1)} async-done(((bf16[16,256,1408]{1,0,2:T(8,128)(2,1)}), bf16[16,256,1408]{1,0,2:T(8,128)(2,1)}, u32[]{:S(2)}, u32[]{:S(2)}) %all-to-all-start) | async-done | bytes 11534368 | tf_op jit(solution)/shard_map/all_to_all | solution.py:16
  362.6 8.5 %all-to-all-start.1 = ((bf16[16,256,1408]{1,0,2:T(8,128)(2,1)}), bf16[16,256,1408]{1,0,2:T(8,128)(2,1)}, u32[]{:S(2)}, u32[]{:S(2)}) async-start(bf16[16,256,1408]{1,0,2:T(8,128)(2,1)} %divide_convert_fusion), calls=%async_computation.1 | async-start | bytes 23068672 | tf_op jit(solution)/shard_map/all_to_all | solution.py:17
  371.1 0.0 copy-done.2
  371.1 0.0 copy-done.3
  371.1 266.0 %all_gather.6 = bf16[2048,16]{0,1:T(8,128)(2,1)S(1)} all-gather(bf16[256,16]{0,1:T(8,128)(2,1)S(1)} %multiply_convert_fusion), channel_id=1, replica_groups=mesh['owner'=4,'rows'=8] {'rows'}, dimensions={0}, use_global_device_ids=true | all-gather | bytes 73728 | tf_op jit(solution)/shard_map/all_gather | solution.py:26
  637.1 5.8 all_gather.7
  642.8 1.4 constant_dynamic-slice_fusion
  644.3 11.3 %copy.20 = bf16[16,8,256,176]{2,1,3,0:T(8,128)(2,1)} copy(bf16[16,8,256,176]{2,0,3,1:T(8,128)(2,1)} %bitcast.2) | data formatting | bytes 23068672 | tf_op jit(solution)/shard_map/all_to_all | solution.py:16
  655.6 18.0 %all_to_all.29 = bf16[16,2048,176]{1,2,0:T(8,128)(2,1)} reshape(bf16[16,8,256,176]{2,1,3,0:T(8,128)(2,1)} %copy.20) | data formatting | bytes 23068672 | tf_op jit(solution)/shard_map/all_to_all | solution.py:16
  673.6 0.0 all-to-all-done.1
  673.6 11.4 %copy.24 = bf16[16,8,256,176]{2,1,3,0:T(8,128)(2,1)} copy(bf16[16,8,256,176]{2,0,3,1:T(8,128)(2,1)} %bitcast.5) | data formatting | bytes 23068672 | tf_op jit(solution)/shard_map/all_to_all | solution.py:17
  685.0 18.0 %all_to_all.33 = bf16[16,2048,176]{1,2,0:T(8,128)(2,1)} reshape(bf16[16,8,256,176]{2,1,3,0:T(8,128)(2,1)} %copy.24) | data formatting | bytes 23068672 | tf_op jit(solution)/shard_map/all_to_all | solution.py:17
  702.9 0.7 copy.30
  (1 shorter events, 0.0 us)
Async XLA Ops:
  7.2 88.2 %all-reduce.3.cloned.1.call-start = ((), (), s32[]{:S(2)}) async-start(), calls=%async_computation.2 | async-start | bytes 360448 | tf_op jit(solution)/shard_map/pmax | solution.py:8
  7.2 14.2 %copy-start = (f32[16,256,1408]{2,1,0:T(8,128)S(1)}, f32[16,256,1408]{2,1,0:T(8,128)}, u32[]{:S(2)}) copy-start(f32[16,256,1408]{2,1,0:T(8,128)} %param.4) | copy-start | bytes 69206016
  110.7 251.8 %all-to-all-start = ((bf16[16,256,1408]{1,0,2:T(8,128)(2,1)}), bf16[16,256,1408]{1,0,2:T(8,128)(2,1)}, u32[]{:S(2)}, u32[]{:S(2)}) async-start(bf16[16,256,1408]{1,0,2:T(8,128)(2,1)} %divide_convert_fusion.1), calls=%async_computation | async-start | bytes 23068672 | tf_op jit(solution)/shard_map/all_to_all | solution.py:16
  117.1 23.7 %copy-start.1 = (f32[16,1408]{1,0:T(8,128)S(1)}, f32[16,1408]{1,0:T(8,128)}, u32[]{:S(2)}) copy-start(f32[16,1408]{1,0:T(8,128)} %get-tuple-element.6) | copy-start | bytes 270340
  141.0 230.1 %copy-start.2 = (f32[256,16]{0,1:T(8,128)S(1)}, f32[256,16]{0,1:T(8,128)}, u32[]{:S(2)}) copy-start(f32[256,16]{0,1:T(8,128)} %param.6) | copy-start | bytes 49156
  141.0 230.1 %copy-start.3 = (f32[256]{0:T(256)S(1)}, f32[256]{0:T(256)}, u32[]{:S(2)}) copy-start(f32[256]{0:T(256)} %param.7) | copy-start | bytes 3076
  362.6 311.0 %all-to-all-start.1 = ((bf16[16,256,1408]{1,0,2:T(8,128)(2,1)}), bf16[16,256,1408]{1,0,2:T(8,128)(2,1)}, u32[]{:S(2)}, u32[]{:S(2)}) async-start(bf16[16,256,1408]{1,0,2:T(8,128)(2,1)} %divide_convert_fusion), calls=%async_computation.1 | async-start | bytes 23068672 | tf_op jit(solution)/shard_map/all_to_all | solution.py:17
Sparse Core Ops, SparseCore 0:
  24.0 71.3 all-reduce.2
where the time goes:
time: 717 us; the launch traced here: 710 us
  blocking collectives  272 us (38%)
  waiting for transfers between devices  255 us (36%)
  local copies, waits for them, and re-layouts  114 us (16%)
  other arithmetic  40.5 us (6%)
  starting transfers between devices  14.9 us (2%)
  between operations  14.1 us (2%)
    all_gather x1, blocking collectives, shards(): row_router = lax.all_gather(part_router, 'rows', axis=0, tiled=True)  266 us
    all_to_all x1, waiting for transfers between devices, shards(): lax.all_to_all(narrow_gate, 'rows', split_axis=2, concat_axis=1, tiled=True)  207 us
    unnamed x11, local copies, waits for them, and re-layouts  52.6 us
    pmax x1, waiting for transfers between devices, shards(): lax.pmax((jnp.max(jnp.abs(master_gate), axis=1), jnp.max(jnp.abs(master_u...  47.8 us
    all_to_all x2, local copies, waits for them, and re-layouts, shards(): lax.all_to_all(narrow_up, 'rows', split_axis=2, concat_axis=1, tiled=True)  29.3 us
    all_to_all x2, local copies, waits for them, and re-layouts, shards(): lax.all_to_all(narrow_gate, 'rows', split_axis=2, concat_axis=1, tiled=True)  29.3 us
  transfers between devices with their start and end apart: 3, of which 2 were waited for; matrix products, arithmetic and copies ran while one was open for 11% of the time, Pallas kernels for 0%

commit v1 on v0

--- a/solution.py
+++ b/solution.py
@@ -1,10 +1,253 @@
+import functools
+
 import jax
 import jax.numpy as jnp
 from jax import lax
+from jax.experimental import pallas as pl
+from jax.experimental.pallas import tpu as pltpu
 from jax.sharding import PartitionSpec as P
 
-
-def shards(master_gate, master_up, router_weight, router_gain):
+MESH = pl.DeviceIdType.MESH
+LANES = 128
+SUBLANES = 8
+PACKED = 16
+SLOTS = 4
+PER_SEND = 2
+VMEM_FOR_BLOCKS = 48 * 1024 * 1024
+
+
+def kernel(
+    owners,
+    peers,
+    gate,
+    up,
+    router,
+    gain,
+    out_gate,
+    out_up,
+    out_router,
+    scales,
+    slots,
+    largest,
+    parts,
+    send,
+    row,
+    slot_sem,
+    send_sem,
+    recv_sem,
+    part_send,
+    part_recv,
+    whole_send,
+    whole_recv,
+    router_send,
+    router_recv,
+):
+    owner, me = lax.axis_index("owner"), lax.axis_index("rows")
+    experts, rows, width = gate.shape
+    tiles = width // LANES
+    cut = width // peers
+    per = parts.shape[1]
+    masters, outs = (gate, up), (out_gate, out_up)
+
+    def fetch(m, e):
+        s = lax.rem(e, SLOTS)
+        return pltpu.make_async_copy(masters[m].at[e], slots.at[m, s], slot_sem.at[m, s])
+
+    for m in range(2):
+        for e in range(SLOTS):
+            fetch(m, e).start()
+
+    lanes = pl.ds(pl.multiple_of(me * rows, LANES), rows)
+    depth = router.shape[0]
+    block = out_router.at[pl.ds(pl.multiple_of(owner * depth, PACKED), depth), lanes]
+    row[...] = (router[...] * gain[...]).astype(row.dtype)
+    flat = owner * peers + me
+    count = owners * peers
+
+    def router_copy(k):
+        to = lax.rem(flat + k, count)
+        return pltpu.make_async_remote_copy(
+            src_ref=row,
+            dst_ref=block,
+            send_sem=router_send.at[k],
+            recv_sem=router_recv.at[k],
+            device_id={"owner": to // peers, "rows": lax.rem(to, peers)},
+            device_id_type=MESH,
+        )
+
+    largest[...] = jnp.zeros_like(largest)
+    for m in range(2):
+
+        def maxima(e, _, m=m):
+            fetch(m, e).wait()
+            k = m * experts + e
+            for c in range(tiles):
+                x = slots[m, lax.rem(e, SLOTS), :, c * LANES : (c + 1) * LANES]
+                largest[(k // SUBLANES) * tiles + c, pl.ds(lax.rem(k, SUBLANES), 1), :] = jnp.max(
+                    jnp.abs(x), axis=0, keepdims=True
+                )
+            fetch(m, lax.rem(e + SLOTS, experts)).start()
+            return 0
+
+        lax.fori_loop(0, experts, maxima, 0)
+
+    def part_copy(k):
+        to = lax.rem(me + k, peers)
+        return pltpu.make_async_remote_copy(
+            src_ref=largest.at[pl.ds(to * per, per)],
+            dst_ref=parts.at[k],
+            send_sem=part_send.at[k],
+            recv_sem=part_recv.at[k],
+            device_id={"rows": to},
+            device_id_type=MESH,
+        )
+
+    mine = scales.at[pl.ds(me * per, per)]
+
+    def whole_copy(k):
+        return pltpu.make_async_remote_copy(
+            src_ref=mine,
+            dst_ref=mine,
+            send_sem=whole_send.at[k],
+            recv_sem=whole_recv.at[k],
+            device_id={"rows": lax.rem(me + k, peers)},
+            device_id_type=MESH,
+        )
+
+    for k in range(1, peers):
+        part_copy(k).start()
+    total = largest[pl.ds(me * per, per)]
+    for k in range(1, peers):
+        part_copy(k).wait_recv()
+        total = jnp.maximum(total, parts[k])
+    mine[...] = total
+    for k in range(1, peers):
+        whole_copy(k).start()
+    for k in range(1, peers):
+        part_copy(k).wait_send()
+    for k in range(1, peers):
+        there = scales.at[pl.ds(lax.rem(me + peers - k, peers) * per, per)]
+        pltpu.make_async_copy(there, there, whole_recv.at[k]).wait()
+    for k in range(1, peers):
+        whole_copy(k).wait_send()
+
+    def send_copy(m, k, e, length):
+        to = lax.rem(me + k, peers)
+        return pltpu.make_async_remote_copy(
+            src_ref=send.at[m, pl.ds(e, length), pl.ds(pl.multiple_of(to * cut, PACKED), cut), :],
+            dst_ref=outs[m].at[pl.ds(e, length), :, lanes],
+            send_sem=send_sem.at[m, k],
+            recv_sem=recv_sem.at[m, k],
+            device_id={"rows": to},
+            device_id_type=MESH,
+        )
+
+    def keep_copy(m, e, length):
+        return pltpu.make_async_copy(
+            send.at[m, pl.ds(e, length), pl.ds(pl.multiple_of(me * cut, PACKED), cut), :],
+            outs[m].at[pl.ds(e, length), :, lanes],
+            send_sem.at[m, 0],
+        )
+
+    order = sorted(range(1, peers), key=lambda k: abs(2 * k - peers))
+    for m in range(2):
+
+        def bulk(step, _, m=m):
+            for i in range(PER_SEND):
+                e = step * PER_SEND + i
+                fetch(m, e).wait()
+                k = m * experts + e
+                for c in range(tiles):
+                    x = slots[m, lax.rem(e, SLOTS), :, c * LANES : (c + 1) * LANES]
+                    s = scales[(k // SUBLANES) * tiles + c, pl.ds(lax.rem(k, SUBLANES), 1), :]
+                    send[m, e, c * LANES : (c + 1) * LANES, :] = (x / s).T.astype(send.dtype)
+
+                @pl.when(e + SLOTS < experts)
+                def _(e=e):
+                    fetch(m, e + SLOTS).start()
+
+            for k in order:
+                send_copy(m, k, step * PER_SEND, PER_SEND).start()
+            keep_copy(m, step * PER_SEND, PER_SEND).start()
+            return 0
+
+        lax.fori_loop(0, experts // PER_SEND, bulk, 0)
+        if m == 0:
+
+            def router_start(k, _):
+                router_copy(k).start()
+                return 0
+
+            lax.fori_loop(1, count, router_start, 0)
+            pltpu.make_async_copy(row, block, router_send.at[0]).start()
+
+    pltpu.make_async_copy(row, block, router_send.at[0]).wait()
+
+    def router_wait(k, _):
+        router_copy(k).wait()
+        return 0
+
+    lax.fori_loop(1, count, router_wait, 0)
+    for m in range(2):
+        keep_copy(m, 0, experts).wait()
+        for k in range(1, peers):
+            send_copy(m, k, 0, experts).wait()
+
+
+def fused(owners, peers, master_gate, master_up, router_weight, router_gain):
+    experts, rows, width = master_gate.shape
+    cut = width // peers
+    tiles = width // LANES
+    groups = 2 * experts // SUBLANES
+    per = -(-groups * tiles // peers)
+    depth = router_weight.shape[1]
+    anywhere = pl.BlockSpec(memory_space=pl.ANY)
+    vmem = pl.BlockSpec(memory_space=pltpu.VMEM)
+    dma = pltpu.SemaphoreType.DMA
+    turned = jax.ShapeDtypeStruct((experts, cut, rows * peers), jnp.bfloat16)
+    gate, up, router, scales = pl.pallas_call(
+        functools.partial(kernel, owners, peers),
+        out_shape=(
+            turned,
+            turned,
+            jax.ShapeDtypeStruct((depth * owners, rows * peers), jnp.bfloat16),
+            jax.ShapeDtypeStruct((per * peers, SUBLANES, LANES), jnp.float32),
+        ),
+        in_specs=[anywhere, anywhere, vmem, vmem],
+        out_specs=(anywhere, anywhere, anywhere, vmem),
+        scratch_shapes=[
+            pltpu.VMEM((2, SLOTS, rows, width), jnp.float32),
+            pltpu.VMEM((per * peers, SUBLANES, LANES), jnp.float32),
+            pltpu.VMEM((peers, per, SUBLANES, LANES), jnp.float32),
+            pltpu.VMEM((2, experts, width, rows), jnp.bfloat16),
+            pltpu.VMEM((depth, rows), jnp.bfloat16),
+            dma((2, SLOTS)),
+            dma((2, peers)),
+            dma((2, peers)),
+            dma((peers,)),
+            dma((peers,)),
+            dma((peers,)),
+            dma((peers,)),
+            dma((owners * peers,)),
+            dma((owners * peers,)),
+        ],
+        compiler_params=pltpu.CompilerParams(
+            has_side_effects=True, vmem_limit_bytes=60 * 1024 * 1024
+        ),
+    )(master_gate, master_up, router_weight.T, router_gain[None, :])
+    scales = scales[: groups * tiles].reshape(2, experts // SUBLANES, tiles, SUBLANES, LANES)
+    scales = scales.transpose(0, 1, 3, 2, 4).reshape(2, experts, width)
+    scales = lax.dynamic_slice_in_dim(scales, lax.axis_index("rows") * cut, cut, axis=2)
+    return (
+        gate.transpose(0, 2, 1),
+        up.transpose(0, 2, 1),
+        scales[0],
+        scales[1],
+        router.T,
+    )
+
+
+def plain(master_gate, master_up, router_weight, router_gain):
     scale_gate, scale_up = lax.pmax(
         (jnp.max(jnp.abs(master_gate), axis=1), jnp.max(jnp.abs(master_up), axis=1)), "rows"
     )
@@ -29,6 +272,23 @@
 
 
 def solution(mesh):
+    owners, peers = mesh.shape["owner"], mesh.shape["rows"]
+
+    def shards(master_gate, master_up, router_weight, router_gain):
+        experts, rows, width = master_gate.shape
+        whole_tiles = (
+            rows % LANES == 0
+            and width % LANES == 0
+            and width % (peers * PACKED) == 0
+            and experts % SUBLANES == 0
+            and experts % SLOTS == 0
+            and experts % PER_SEND == 0
+            and router_weight.shape[1] % PACKED == 0
+            and (4 * experts + 8 * SLOTS) * rows * width <= VMEM_FOR_BLOCKS
+        )
+        run = functools.partial(fused, owners, peers) if whole_tiles else plain
+        return run(master_gate, master_up, router_weight, router_gain)
+
     return jax.shard_map(
         shards,
         mesh=mesh,

time: 717 us -> 558 us (0.78)
  Pallas kernels: 0 us -> 538 us
  blocking collectives: 272 us -> 0 us
  waiting for transfers between devices: 255 us -> 0 us
  local copies, waits for them, and re-layouts: 114 us -> 18.3 us
  other arithmetic: 40.5 us -> 0.01 us
  starting transfers between devices: 14.9 us -> 0 us
  between operations: 14.1 us -> 0.68 us
    pallas_call x0 -> x1, Pallas kernels: none -> 538 us  [fused(): pl.pallas_call(functools.partial(kernel, owners, peers), out_shape=(turne...]
    all_gather x2 -> x0, blocking collectives: 272 us -> none  [the longest x1 266 us: shards(): row_router = lax.all_gather(part_router, 'rows', axis=0, tiled=True)]
    all_to_all x2 -> x0, waiting for transfers between devices: 207 us -> none  [the longest x1 207 us: shards(): lax.all_to_all(narrow_gate, 'rows', split_axis=2, concat_axis=1, tiled=True)]
    all_to_all x4 -> x0, local copies, waits for them, and re-layouts: 58.6 us -> none  [the longest x2 29.3 us: shards(): lax.all_to_all(narrow_up, 'rows', split_axis=2, concat_axis=1, tiled=True)]
    pmax x1 -> x0, waiting for transfers between devices: 47.8 us -> none  [shards(): lax.pmax((jnp.max(jnp.abs(master_gate), axis=1), jnp.max(jnp.abs(master_u...]
    unnamed x11, local copies, waits for them, and re-layouts: 52.6 us -> 16.5 us
    convert_element_type x3 -> x0, other arithmetic: 28.4 us -> none  [the longest x1 14.2 us: shards(): (master_gate / jnp.expand_dims(scale_gate, 1)).astype(jnp.bfloat16)]
    all_to_all x2 -> x0, starting transfers between devices: 14.9 us -> none  [the longest x1 8.54 us: shards(): lax.all_to_all(narrow_up, 'rows', split_axis=2, concat_axis=1, tiled=True)]
  transfers between devices with their start and end apart: 3 -> 0, of which waited for: 2 -> 0; matrix products, arithmetic and copies ran while one was open for 11% -> 0% of each run, Pallas kernels for 0% -> 0%
where the time goes in v1:
time: 558 us; the launch traced here: 557 us
  Pallas kernels  538 us (96%)
  local copies, waits for them, and re-layouts  18.3 us (3%)
    pallas_call x1, Pallas kernels, fused(): pl.pallas_call(functools.partial(kernel, owners, peers), out_shape=(turne...  538 us
    unnamed x11, local copies, waits for them, and re-layouts  16.5 us

profile of v1, /device:TPU:14, one launch (start us, length us, event | category | flops | bytes accessed | tf_op | source)
XLA Modules:
  0.0 556.6 jit_solution(14742260075287049138)
XLA Ops:
  0.6 537.6 %shard_map.83 = (bf16[16,176,2048]{2,1,0:T(8,128)(2,1)}, bf16[16,176,2048]{2,1,0:T(8,128)(2,1)}, bf16[64,2048]{1,0:T(8,128)(2,1)}, f32[48,8,128]{2,1,0:T(8,128)}) custom-call(f32[16,256,1408]{2,1,0:T(8,128)} %gate.1, f32[16,256,1408]{2,1,0:T(8,128)} %up.1, f32[16,256]{1,0:T(8,128)} %bitcast.20, f32[1,256]{1,0:T(1,128)} %bitcast.21), custom_call_target="tpu_custom_call" | custom-call | tf_op jit(solution)/shard_map/pallas_call | solution.py:208
  538.3 0.0 slice-start
  538.3 1.1 slice.9
  539.4 0.7 dynamic-slice_bitcast_fusion
  540.1 0.0 slice-start.1
  540.1 0.0 slice-start.2
  540.1 11.3 %copy.12 = bf16[16,2048,176]{1,2,0:T(8,128)(2,1)} copy(bf16[16,2048,176]{1,2,0:T(8,128)(2,1)} %bitcast.17) | data formatting | bytes 23068672
  551.4 0.0 slice-done
  551.4 0.0 slice-done.1
  551.4 0.0 slice-done.2
  551.4 0.0 copy-start
  551.4 4.4 copy.13
  555.9 0.0 copy-done
  555.9 0.7 copy.14
  (1 shorter events, 0.0 us)
Async XLA Ops:
  538.3 13.1 %slice-start = ((s8[11534336]{0:T(1024)(128)(4,1)}), s8[3145728]{0:T(1024)(128)(4,1)S(1)}, s32[]{:S(2)}) async-start(s8[11534336]{0:T(1024)(128)(4,1)} %bitcast.14), calls=%async_computation | async-start | bytes 6291456
  540.1 11.3 %slice-start.1 = ((s8[11534336]{0:T(1024)(128)(4,1)}), s8[4194304]{0:T(1024)(128)(4,1)S(1)}, s32[]{:S(2)}) async-start(s8[11534336]{0:T(1024)(128)(4,1)} %bitcast.14), calls=%async_computation.1 | async-start | bytes 8388608
  540.1 11.3 %slice-start.2 = ((s8[11534336]{0:T(1024)(128)(4,1)}), s8[4194304]{0:T(1024)(128)(4,1)S(1)}, s32[]{:S(2)}) async-start(s8[11534336]{0:T(1024)(128)(4,1)} %bitcast.14), calls=%async_computation.2 | async-start | bytes 8388608
  551.4 4.4 copy-start

commit v2 on v1

v2 whole, which is shorter than its diff:
```python
import functools

import jax
import jax.numpy as jnp
from jax import lax
from jax.experimental import pallas as pl
from jax.experimental.pallas import tpu as pltpu
from jax.sharding import PartitionSpec as P

MESH = pl.DeviceIdType.MESH
LANES = 128
SUBLANES = 8
PACKED = 16
SLOTS = 4
PER_SEND = 2
VMEM_FOR_BLOCKS = 48 * 1024 * 1024
VMEM_FOR_REST = 2 * 1024 * 1024


def kernel(
    owners,
    peers,
    gate,
    up,
    router,
    gain,
    out_gate,
    out_up,
    out_router,
    scales_first,
    scales_rest,
    slots,
    largest_first,
    largest_rest,
    parts_first,
    parts_rest,
    send,
    row,
    slot_sem,
    send_sem,
    recv_sem,
    part_send,
    part_recv,
    whole_send,
    whole_recv,
    router_send,
    router_recv,
):
    owner, me = lax.axis_index("owner"), lax.axis_index("rows")
    experts, rows, width = gate.shape
    tiles = width // LANES
    cut = width // peers
    masters, outs = (gate, up), (out_gate, out_up)
    largest, parts = (largest_first, largest_rest), (parts_first, parts_rest)
    scales = (scales_first, scales_rest)
    lanes = pl.ds(pl.multiple_of(me * rows, LANES), rows)

    def fetch(m, first, i):
        s = lax.rem(i, SLOTS)
        return pltpu.make_async_copy(masters[m].at[first + i], slots.at[s], slot_sem.at[s])

    def begin(m, first, length):
        for i in range(min(SLOTS, length)):
            fetch(m, first, i).start()

    def advance(m, first, length, i):
        if length > SLOTS:

            @pl.when(i + SLOTS < length)
            def _():
                fetch(m, first, i + SLOTS).start()

    def place(m, e, c, first):
        k = m * experts + e - (0 if first else SUBLANES)
        return (k // SUBLANES) * tiles + c, pl.ds(lax.rem(k, SUBLANES), 1)

    def maxima(m, first, length):
        stage = 0 if m == 0 and first < SUBLANES else 1

        def body(i, _):
            fetch(m, first, i).wait()
            for c in range(tiles):
                x = slots[lax.rem(i, SLOTS), :, c * LANES : (c + 1) * LANES]
                tile, sub = place(m, first + i, c, stage == 0)
                largest[stage][tile, sub, :] = jnp.max(jnp.abs(x), axis=0, keepdims=True)
            advance(m, first, length, i)
            return 0

        lax.fori_loop(0, length, body, 0)

    def part_copy(stage, k):
        per = parts[stage].shape[1]
        to = lax.rem(me + k, peers)
        return pltpu.make_async_remote_copy(
            src_ref=largest[stage].at[pl.ds(to * per, per)],
            dst_ref=parts[stage].at[k],
            send_sem=part_send.at[stage, k],
            recv_sem=part_recv.at[stage, k],
            device_id={"rows": to},
            device_id_type=MESH,
        )

    def share(stage, of):
        per = parts[stage].shape[1]
        return scales[stage].at[pl.ds(of * per, per)]

    def whole_copy(stage, k):
        return pltpu.make_async_remote_copy(
            src_ref=share(stage, me),
            dst_ref=share(stage, me),
            send_sem=whole_send.at[stage, k],
            recv_sem=whole_recv.at[stage, k],
            device_id={"rows": lax.rem(me + k, peers)},
            device_id_type=MESH,
        )

    order = sorted(range(1, peers), key=lambda k: abs(2 * k - peers))

    def scatter(stage):
        for k in order:
            part_copy(stage, k).start()

    def reduce(stage):
        per = parts[stage].shape[1]
        total = largest[stage][pl.ds(me * per, per)]
        for k in order:
            part_copy(stage, k).wait_recv()
            total = jnp.maximum(total, parts[stage][k])
        share(stage, me)[...] = total
        for k in order:
            whole_copy(stage, k).start()

    def gathered(stage):
        for k in order:
            part_copy(stage, k).wait_send()
            there = share(stage, lax.rem(me + peers - k, peers))
            pltpu.make_async_copy(there, there, whole_recv.at[stage, k]).wait()
            whole_copy(stage, k).wait_send()

    def send_copy(m, k, e, length):
        to = lax.rem(me + k, peers)
        return pltpu.make_async_remote_copy(
            src_ref=send.at[m, pl.ds(e, length), pl.ds(pl.multiple_of(to * cut, PACKED), cut), :],
            dst_ref=outs[m].at[pl.ds(e, length), :, lanes],
            send_sem=send_sem.at[m, k],
            recv_sem=recv_sem.at[m, k],
            device_id={"rows": to},
            device_id_type=MESH,
        )

    def keep_copy(m, e, length):
        return pltpu.make_async_copy(
            send.at[m, pl.ds(e, length), pl.ds(pl.multiple_of(me * cut, PACKED), cut), :],
            outs[m].at[pl.ds(e, length), :, lanes],
            send_sem.at[m, 0],
        )

    def bulk(m, first, length, batch):
        stage = 0 if m == 0 and first < SUBLANES else 1

        def body(step, _):
            for j in range(batch):
                i = step * batch + j
                fetch(m, first, i).wait()
                for c in range(tiles):
                    x = slots[lax.rem(i, SLOTS), :, c * LANES : (c + 1) * LANES]
                    tile, sub = place(m, first + i, c, stage == 0)
                    s = scales[stage][tile, sub, :]
                    send[m, first + i, c * LANES : (c + 1) * LANES, :] = (x / s).T.astype(send.dtype)
                advance(m, first, length, i)
            for k in order:
                send_copy(m, k, first + step * batch, batch).start()
            keep_copy(m, first + step * batch, batch).start()
            return 0

        lax.fori_loop(0, length // batch, body, 0)

    depth = router.shape[0]
    block = out_router.at[pl.ds(pl.multiple_of(owner * depth, PACKED), depth), lanes]
    flat = owner * peers + me
    count = owners * peers

    def router_copy(k):
        to = lax.rem(flat + k, count)
        return pltpu.make_async_remote_copy(
            src_ref=row,
            dst_ref=block,
            send_sem=router_send.at[k],
            recv_sem=router_recv.at[k],
            device_id={"owner": to // peers, "rows": lax.rem(to, peers)},
            device_id_type=MESH,
        )

    def router_start(k, _):
        router_copy(k).start()
        return 0

    def router_wait(k, _):
        router_copy(k).wait()
        return 0

    begin(0, 0, SUBLANES)
    largest_first[...] = jnp.zeros_like(largest_first)
    largest_rest[...] = jnp.zeros_like(largest_rest)
    row[...] = (router[...] * gain[...]).astype(row.dtype)
    maxima(0, 0, SUBLANES)
    scatter(0)
    begin(0, 0, 2)
    reduce(0)
    gathered(0)
    bulk(0, 0, 2, 1)
    if experts > SUBLANES:
        begin(0, SUBLANES, experts - SUBLANES)
        maxima(0, SUBLANES, experts - SUBLANES)
    begin(1, 0, experts)
    maxima(1, 0, experts)
    scatter(1)
    begin(0, 2, 2)
    bulk(0, 2, 2, 2)
    begin(0, 4, SUBLANES - 4)
    reduce(1)
    bulk(0, 4, SUBLANES - 4, PER_SEND)
    if experts > SUBLANES:
        begin(0, SUBLANES, experts - SUBLANES)
    gathered(1)
    if experts > SUBLANES:
        bulk(0, SUBLANES, experts - SUBLANES, PER_SEND)
    begin(1, 0, experts)
    lax.fori_loop(1, count, router_start, 0)
    keep_router = pltpu.make_async_copy(row, block, router_send.at[0])
    keep_router.start()
    bulk(1, 0, experts, PER_SEND)

    keep_router.wait()
    lax.fori_loop(1, count, router_wait, 0)
    for m in range(2):
        keep_copy(m, 0, experts).wait()
        for k in range(1, peers):
            send_copy(m, k, 0, experts).wait()


def land(*refs):
    arrays = len(refs) // 2
    ins, outs, sem = refs[:arrays], refs[arrays:-1], refs[-1]
    copies = [pltpu.make_async_copy(a, b, sem.at[i]) for i, (a, b) in enumerate(zip(ins, outs))]
    for copy in copies:
        copy.start()
    for copy in copies:
        copy.wait()


def fused(owners, peers, master_gate, master_up, router_weight, router_gain):
    experts, rows, width = master_gate.shape
    cut = width // peers
    tiles = width // LANES
    groups = 2 * experts // SUBLANES
    first, rest = -(-tiles // peers), -(-(groups - 1) * tiles // peers)
    depth = router_weight.shape[1]
    anywhere = pl.BlockSpec(memory_space=pl.ANY)
    vmem = pl.BlockSpec(memory_space=pltpu.VMEM)
    dma = pltpu.SemaphoreType.DMA
    turned = jax.ShapeDtypeStruct((experts, cut, rows * peers), jnp.bfloat16)

    def maxima(*shape):
        return (*shape, SUBLANES, LANES)

    gate, up, router, scales_first, scales_rest = pl.pallas_call(
        functools.partial(kernel, owners, peers),
        out_shape=(
            turned,
            turned,
            jax.ShapeDtypeStruct((depth * owners, rows * peers), jnp.bfloat16),
            jax.ShapeDtypeStruct(maxima(first * peers), jnp.float32),
            jax.ShapeDtypeStruct(maxima(rest * peers), jnp.float32),
        ),
        in_specs=[anywhere, anywhere, vmem, vmem],
        out_specs=(anywhere, anywhere, anywhere, vmem, vmem),
        scratch_shapes=[
            pltpu.VMEM((SLOTS, rows, width), jnp.float32),
            pltpu.VMEM(maxima(first * peers), jnp.float32),
            pltpu.VMEM(maxima(rest * peers), jnp.float32),
            pltpu.VMEM(maxima(peers, first), jnp.float32),
            pltpu.VMEM(maxima(peers, rest), jnp.float32),
            pltpu.VMEM((2, experts, width, rows), jnp.bfloat16),
            pltpu.VMEM((depth, rows), jnp.bfloat16),
            dma((SLOTS,)),
            dma((2, peers)),
            dma((2, peers)),
            dma((2, peers)),
            dma((2, peers)),
            dma((2, peers)),
            dma((2, peers)),
            dma((owners * peers,)),
            dma((owners * peers,)),
        ],
        compiler_params=pltpu.CompilerParams(
            has_side_effects=True,
            vmem_limit_bytes=(4 * experts + 4 * SLOTS) * rows * width + VMEM_FOR_REST,
        ),
    )(master_gate, master_up, router_weight.T, router_gain[None, :])
    landed = (gate, up, router, scales_first, scales_rest)
    gate, up, router, scales_first, scales_rest = pl.pallas_call(
        land,
        out_shape=[jax.ShapeDtypeStruct(a.shape, a.dtype) for a in landed],
        in_specs=[anywhere] * len(landed),
        out_specs=[pl.BlockSpec(memory_space=pltpu.HBM)] * len(landed),
        scratch_shapes=[dma((len(landed),))],
        compiler_params=pltpu.CompilerParams(vmem_limit_bytes=VMEM_FOR_REST),
        cost_estimate=pl.CostEstimate(
            flops=0, bytes_accessed=2 * sum(a.size for a in landed), transcendentals=0
        ),
    )(*landed)
    scales = jnp.concatenate([scales_first[:tiles], scales_rest[: (groups - 1) * tiles]])
    scales = scales.reshape(2, experts // SUBLANES, tiles, SUBLANES, LANES)
    scales = scales.transpose(0, 1, 3, 2, 4).reshape(2, experts, width)
    scales = lax.dynamic_slice_in_dim(scales, lax.axis_index("rows") * cut, cut, axis=2)
    return (
        gate.transpose(0, 2, 1),
        up.transpose(0, 2, 1),
        scales[0],
        scales[1],
        router.T,
    )


def plain(master_gate, master_up, router_weight, router_gain):
    scale_gate, scale_up = lax.pmax(
        (jnp.max(jnp.abs(master_gate), axis=1), jnp.max(jnp.abs(master_up), axis=1)), "rows"
    )
    narrow_gate, narrow_up = (
        (master_gate / jnp.expand_dims(scale_gate, 1)).astype(jnp.bfloat16),
        (master_up / jnp.expand_dims(scale_up, 1)).astype(jnp.bfloat16),
    )
    final_gate, final_up = (
        lax.all_to_all(narrow_gate, "rows", split_axis=2, concat_axis=1, tiled=True),
        lax.all_to_all(narrow_up, "rows", split_axis=2, concat_axis=1, tiled=True),
    )
    scale_gate = lax.dynamic_slice_in_dim(
        scale_gate, lax.axis_index("rows") * final_gate.shape[2], final_gate.shape[2], axis=1
    )
    scale_up = lax.dynamic_slice_in_dim(
        scale_up, lax.axis_index("rows") * final_up.shape[2], final_up.shape[2], axis=1
    )
    part_router = (router_weight * router_gain[:, None]).astype(jnp.bfloat16)
    row_router = lax.all_gather(part_router, "rows", axis=0, tiled=True)
    serve_router = lax.all_gather(row_router, "owner", axis=1, tiled=True)
    return (final_gate, final_up, scale_gate, scale_up, serve_router)


def solution(mesh):
    owners, peers = mesh.shape["owner"], mesh.shape["rows"]

    def shards(master_gate, master_up, router_weight, router_gain):
        experts, rows, width = master_gate.shape
        whole_tiles = (
            rows % LANES == 0
            and width % LANES == 0
            and width % (peers * PACKED) == 0
            and experts % SUBLANES == 0
            and experts >= SLOTS
            and experts % PER_SEND == 0
            and router_weight.shape[1] % PACKED == 0
            and (4 * experts + 4 * SLOTS) * rows * width <= VMEM_FOR_BLOCKS
        )
        run = functools.partial(fused, owners, peers) if whole_tiles else plain
        return run(master_gate, master_up, router_weight, router_gain)

    return jax.shard_map(
        shards,
        mesh=mesh,
        in_specs=(
            P("owner", "rows", None),
            P("owner", "rows", None),
            P("rows", "owner"),
            P("rows"),
        ),
        out_specs=(
            P("owner", None, "rows"),
            P("owner", None, "rows"),
            P("owner", "rows"),
            P("owner", "rows"),
            P(),
        ),
        check_vma=False,
    )
```

time: 558 us -> 542 us (0.971)
  local copies, waits for them, and re-layouts: 18.3 us -> 2.1 us
    unnamed x11 -> x4, local copies, waits for them, and re-layouts: 16.5 us -> 1.39 us
    pallas_call x0 -> x1, Pallas kernels: none -> 8.28 us  [fused(): pl.pallas_call(land, out_shape=[jax.ShapeDtypeStruct(a.shape, a.dtype) fo...]
    pallas_call x1, Pallas kernels: 538 us -> 530 us  [fused(): pl.pallas_call(functools.partial(kernel, owners, peers), out_shape=(turne...]
where the time goes in v2:
time: 542 us
  Pallas kernels  539 us (99%)
    pallas_call x1, Pallas kernels, fused(): pl.pallas_call(functools.partial(kernel, owners, peers), out_shape=(turne...  530 us

profile of v2, /device:TPU:14, one launch (start us, length us, event | category | flops | bytes accessed | tf_op | source)
XLA Modules:
  0.0 541.6 jit_solution(10968205708915756441)
XLA Ops:
  0.6 0.0 copy-start
  0.6 0.7 copy-done
  1.4 0.0 copy-start.1
  1.4 0.7 copy-done.1
  2.0 530.5 %shard_map.83 = (bf16[16,176,2048]{2,1,0:T(8,128)(2,1)S(1)}, bf16[16,176,2048]{2,1,0:T(8,128)(2,1)S(1)}, bf16[64,2048]{1,0:T(8,128)(2,1)S(1)}, f32[16,8,128]{2,1,0:T(8,128)S(1)}, f32[40,8,128]{2,1,0:T(8,128)S(1)}) custom-call(f32[16,256,1408]{2,1,0:T(8,128)} %gate.1, f32[16,256,1408]{2,1,0:T(8,128)} %up.1, f32[16,256]{1,0:T(8,128)S(1)} %bitcast.14, ...), custom_call_target="tpu_custom_call" | custom-call | tf_op jit(solution)/shard_map/pallas_call | solution.py:267
  532.5 8.3 %shard_map.84 = (bf16[16,176,2048]{2,1,0:T(8,128)(2,1)}, bf16[16,176,2048]{2,1,0:T(8,128)(2,1)}, bf16[64,2048]{1,0:T(8,128)(2,1)}, f32[16,8,128]{2,1,0:T(8,128)S(1)}, f32[40,8,128]{2,1,0:T(8,128)S(1)}) custom-call(bf16[16,176,2048]{2,1,0:T(8,128)(2,1)S(1)} %get-tuple-element.15.refs_0_, bf16[16,176,2048]{2,1,0:T(8,128)(2,1)S(1)} %get-tuple-element.16.refs_1_, ...), custom_call_target="tpu_custom_call" | custom-call | bytes 23445504 | tf_op jit(solution)/shard_map/pallas_call | solution.py:302
  540.9 0.7 dynamic-slice_bitcast_fusion
  (3 shorter events, 0.0 us)
Async XLA Ops:
  0.6 0.7 copy-start
  1.4 0.7 copy-start.1

commit v3 on v2

--- a/solution.py
+++ b/solution.py
@@ -55,6 +55,17 @@
     scales = (scales_first, scales_rest)
     lanes = pl.ds(pl.multiple_of(me * rows, LANES), rows)
 
+    pairs = peers & (peers - 1) == 0
+
+    def partner(k):
+        if not pairs:
+            return lax.rem(me + k, peers)
+        bits = [1 << b for b in range(peers.bit_length() - 1) if k >> b & 1]
+        return sum((bit - 2 * bit * lax.rem(me // bit, 2) for bit in bits), me)
+
+    def origin(k):
+        return partner(k) if pairs else lax.rem(me + peers - k, peers)
+
     def fetch(m, first, i):
         s = lax.rem(i, SLOTS)
         return pltpu.make_async_copy(masters[m].at[first + i], slots.at[s], slot_sem.at[s])
@@ -90,7 +101,7 @@
 
     def part_copy(stage, k):
         per = parts[stage].shape[1]
-        to = lax.rem(me + k, peers)
+        to = partner(k)
         return pltpu.make_async_remote_copy(
             src_ref=largest[stage].at[pl.ds(to * per, per)],
             dst_ref=parts[stage].at[k],
@@ -110,11 +121,11 @@
             dst_ref=share(stage, me),
             send_sem=whole_send.at[stage, k],
             recv_sem=whole_recv.at[stage, k],
-            device_id={"rows": lax.rem(me + k, peers)},
+            device_id={"rows": partner(k)},
             device_id_type=MESH,
         )
 
-    order = sorted(range(1, peers), key=lambda k: abs(2 * k - peers))
+    order = sorted(range(1, peers), key=lambda k: (k.bit_length(), k))
 
     def scatter(stage):
         for k in order:
@@ -133,12 +144,12 @@
     def gathered(stage):
         for k in order:
             part_copy(stage, k).wait_send()
-            there = share(stage, lax.rem(me + peers - k, peers))
+            there = share(stage, origin(k))
             pltpu.make_async_copy(there, there, whole_recv.at[stage, k]).wait()
             whole_copy(stage, k).wait_send()
 
     def send_copy(m, k, e, length):
-        to = lax.rem(me + k, peers)
+        to = partner(k)
         return pltpu.make_async_remote_copy(
             src_ref=send.at[m, pl.ds(e, length), pl.ds(pl.multiple_of(to * cut, PACKED), cut), :],
             dst_ref=outs[m].at[pl.ds(e, length), :, lanes],
@@ -199,11 +210,25 @@
         router_copy(k).wait()
         return 0
 
+    barrier = pltpu.get_barrier_semaphore()
+
+    def greet(k, _):
+        to = lax.rem(flat + k, count)
+        pl.semaphore_signal(
+            barrier,
+            inc=1,
+            device_id={"owner": to // peers, "rows": lax.rem(to, peers)},
+            device_id_type=MESH,
+        )
+        return 0
+
     begin(0, 0, SUBLANES)
+    lax.fori_loop(1, count, greet, 0)
     largest_first[...] = jnp.zeros_like(largest_first)
     largest_rest[...] = jnp.zeros_like(largest_rest)
     row[...] = (router[...] * gain[...]).astype(row.dtype)
     maxima(0, 0, SUBLANES)
+    pl.semaphore_wait(barrier, count - 1)
     scatter(0)
     begin(0, 0, 2)
     reduce(0)
@@ -294,6 +319,7 @@
             dma((owners * peers,)),
         ],
         compiler_params=pltpu.CompilerParams(
+            collective_id=0,
             has_side_effects=True,
             vmem_limit_bytes=(4 * experts + 4 * SLOTS) * rows * width + VMEM_FOR_REST,
         ),

time: 542 us -> 536 us (0.989)
  Pallas kernels: 539 us -> 533 us
    pallas_call x1, Pallas kernels: 530 us -> 525 us  [fused(): pl.pallas_call(functools.partial(kernel, owners, peers), out_shape=(turne...]
where the time goes in v3:
time: 536 us
  Pallas kernels  533 us (99%)
    pallas_call x1, Pallas kernels, fused(): pl.pallas_call(functools.partial(kernel, owners, peers), out_shape=(turne...  525 us

profile of v3, /device:TPU:14, one launch (start us, length us, event | category | flops | bytes accessed | tf_op | source)
XLA Modules:
  0.0 535.7 jit_solution(1459124681674416077)
XLA Ops:
  0.6 0.0 copy-start
  0.6 0.7 copy-done
  1.4 0.0 copy-start.1
  1.4 0.7 copy-done.1
  2.0 524.6 %shard_map.83 = (bf16[16,176,2048]{2,1,0:T(8,128)(2,1)S(1)}, bf16[16,176,2048]{2,1,0:T(8,128)(2,1)S(1)}, bf16[64,2048]{1,0:T(8,128)(2,1)S(1)}, f32[16,8,128]{2,1,0:T(8,128)S(1)}, f32[40,8,128]{2,1,0:T(8,128)S(1)}) custom-call(f32[16,256,1408]{2,1,0:T(8,128)} %gate.1, f32[16,256,1408]{2,1,0:T(8,128)} %up.1, f32[16,256]{1,0:T(8,128)S(1)} %bitcast.14, ...), custom_call_target="tpu_custom_call" | custom-call | tf_op jit(solution)/shard_map/pallas_call | solution.py:292
  526.7 8.3 %shard_map.84 = (bf16[16,176,2048]{2,1,0:T(8,128)(2,1)}, bf16[16,176,2048]{2,1,0:T(8,128)(2,1)}, bf16[64,2048]{1,0:T(8,128)(2,1)}, f32[16,8,128]{2,1,0:T(8,128)S(1)}, f32[40,8,128]{2,1,0:T(8,128)S(1)}) custom-call(bf16[16,176,2048]{2,1,0:T(8,128)(2,1)S(1)} %get-tuple-element.15.refs_0_, bf16[16,176,2048]{2,1,0:T(8,128)(2,1)S(1)} %get-tuple-element.16.refs_1_, ...), custom_call_target="tpu_custom_call" | custom-call | bytes 23445504 | tf_op jit(solution)/shard_map/pallas_call | solution.py:328
  535.0 0.7 dynamic-slice_bitcast_fusion
  (3 shorter events, 0.0 us)
Async XLA Ops:
  0.6 0.7 copy-start
  1.4 0.7 copy-start.1
